TPU v7x, 32 devices: a whole 2x2x4 slice. The times are simulated.
32 devices in a mesh: dp: 8 (over z, x), ctx: 4 (over y, core).
Axes of the slice: x: 2, y: 2, z: 4, core: 2. Of those that a mesh axis runs over, the one named last changes fastest.
Arguments:
- tokens: bfloat16 [8192, 1536], P(('dp', 'ctx')), may hold values from -6 to 6
- norm_attn: float32 [1536], P(('dp', 'ctx')), may hold values from 0.5 to 1.5
- w_qkv: bfloat16 [3072, 1536], P(('dp', 'ctx')), may hold values from -1 to 1
- w_out: bfloat16 [1536, 1536], P(('dp', 'ctx')), may hold values from -0.875 to 0.875
- norm_mlp: float32 [1536], P(('dp', 'ctx')), may hold values from 0.5 to 1.5
- w_gate_up: bfloat16 [8192, 1536], P(('dp', 'ctx')), may hold values from -0.15625 to 0.15625
- w_down: bfloat16 [1536, 4096], P(('dp', 'ctx')), may hold values from -0.09375 to 0.09375
- cotangent: bfloat16 [8192, 1536], P(('dp', 'ctx')), may hold values from -6 to 6
- seq_lengths: int32 [8, 2], P('dp'), may hold values from 1 to 768, 1024 in all within a row
- block_slot: int32 [8, 8], P('dp'), may hold values from 0 to 7, each once within a row
Outputs:
- result: bfloat16 [8192, 1536], P(('dp', 'ctx'))
- grad_input: float32 [8192, 1536], P(('dp', 'ctx'))
- grad_norm_attn: float32 [1536], P(('dp', 'ctx'))
- grad_qkv: float32 [3072, 1536], P(('dp', 'ctx'))
- grad_out: float32 [1536, 1536], P(('dp', 'ctx'))
- grad_norm_mlp: float32 [1536], P(('dp', 'ctx'))
- grad_gate_up: float32 [8192, 1536], P(('dp', 'ctx'))
- grad_down: float32 [1536, 4096], P(('dp', 'ctx'))
Inputs may be any that keep to these rules, and one draw needn't show every extreme that they name: `seq_lengths`: each row sums to 1024. `block_slot`: each row names every number once; ctx device c of group g holds the blocks of positions c * 2 to (c + 1) * 2 - 1 of that row.
All inputs are finite; a program needn't handle non-finite values.
Results may differ from a plain program's by a relative error of at most 0.025.
Values may be sent and summed in bfloat16 or wider, within the bound.
A program may use at most 320 MiB of HBM per device.

v0:
```python
import math
import jax
import jax.numpy as jnp
from jax import lax
from jax.sharding import PartitionSpec as P

QUERY_HEADS = 16
KEY_VALUE_HEADS = 8
HEAD_SIZE = 96
FF = 4096
BLK = 128
QUERY_FEATURES = 1536
KEY_FEATURES = 768
EPSILON = 1e-05
THETA = 100000.0
MASK_FILL = -1e30


def rope_tables(rope_pos):
    half_dim = HEAD_SIZE // 2
    exponent = jnp.arange(half_dim, dtype=jnp.float32) * (2.0 / HEAD_SIZE)
    frequency = jnp.power(jnp.float32(THETA), -exponent)
    angles = rope_pos.astype(jnp.float32)[:, None] * frequency[None, :]
    return (jnp.cos(angles)[:, None, :], jnp.sin(angles)[:, None, :])


def apply_rotation(values, cosine_table, sine_values):
    half_dim = HEAD_SIZE // 2
    first_half = values[..., :half_dim]
    second_half = values[..., half_dim:]
    return jnp.concatenate(
        [
            first_half * cosine_table - second_half * sine_values,
            second_half * cosine_table + first_half * sine_values,
        ],
        -1,
    )


def rotate_back(gradient, cosine_table, sine_values):
    half_dim = HEAD_SIZE // 2
    first_half = gradient[..., :half_dim]
    second_half = gradient[..., half_dim:]
    return jnp.concatenate(
        [
            first_half * cosine_table + second_half * sine_values,
            second_half * cosine_table - first_half * sine_values,
        ],
        -1,
    )


def positions(lengths, slot_table, first_row, count_of_rows):
    row_index = first_row + jnp.arange(count_of_rows, dtype=jnp.int32)
    block_index = row_index // BLK
    lookup = jnp.arange(slot_table.shape[0], dtype=jnp.int32)
    slot_of = jnp.sum(jnp.where(block_index[:, None] == lookup[None, :], slot_table[None, :], 0), 1)
    stream = slot_of * BLK + row_index % BLK
    seq_ends = jnp.cumsum(lengths)
    passed = stream[:, None] >= seq_ends[None, :]
    segment = jnp.sum(passed.astype(jnp.int32), 1)
    offset = jnp.sum(jnp.where(passed, seq_ends[None, :], 0), 1)
    return (stream, segment, stream - offset)


def norm_back(grad_normed, gain, source, scale):
    weighted = grad_normed * gain
    return scale * weighted - source * scale**3 * jnp.mean(weighted * source, -1, keepdims=True)


def full_product(left_side, whole_weight):
    return jnp.dot(left_side, whole_weight.T, preferred_element_type=jnp.float32)


def full_back(grad_side, whole_weight):
    return jnp.dot(grad_side, whole_weight, preferred_element_type=jnp.float32)


def owned_three(first_part, second_part, third_part):
    return (
        lax.psum_scatter(first_part, ("dp", "ctx"), scatter_dimension=0, tiled=True),
        lax.psum_scatter(second_part, ("dp", "ctx"), scatter_dimension=0, tiled=True),
        lax.psum_scatter(third_part, ("dp", "ctx"), scatter_dimension=0, tiled=True),
    )


def shards(
    tokens, norm_attn, w_qkv, w_out, norm_mlp, w_gate_up, w_down, cotangent, seq_lengths, block_slot
):
    count_of_rows = tokens.shape[0]
    ctx_place = lax.axis_index("ctx")
    lengths = seq_lengths[0]
    slot_table = block_slot[0]
    heads_ratio = QUERY_HEADS // KEY_VALUE_HEADS
    score_scale = 1.0 / math.sqrt(HEAD_SIZE)
    stream, segment, rope_pos = positions(
        lengths, slot_table, ctx_place * count_of_rows, count_of_rows
    )
    cosine_table, sine_values = rope_tables(rope_pos)
    gain_one, gain_two = (
        lax.all_gather(norm_attn, ("dp", "ctx"), axis=0, tiled=True),
        lax.all_gather(norm_mlp, ("dp", "ctx"), axis=0, tiled=True),
    )
    qkv_full, out_full = (
        lax.all_gather(w_qkv, ("dp", "ctx"), axis=0, tiled=True),
        lax.all_gather(w_out, ("dp", "ctx"), axis=0, tiled=True),
    )
    source = tokens.astype(jnp.float32)
    scale_one = lax.rsqrt(jnp.mean(source * source, -1, keepdims=True) + EPSILON)
    normed_one = (source * scale_one * gain_one).astype(jnp.bfloat16)
    projected_output = full_product(normed_one, qkv_full)
    query_rows = apply_rotation(
        projected_output[:, :QUERY_FEATURES].reshape(count_of_rows, QUERY_HEADS, HEAD_SIZE),
        cosine_table,
        sine_values,
    ).astype(jnp.bfloat16)
    keys_mine = apply_rotation(
        projected_output[:, QUERY_FEATURES : QUERY_FEATURES + KEY_FEATURES].reshape(
            count_of_rows, KEY_VALUE_HEADS, HEAD_SIZE
        ),
        cosine_table,
        sine_values,
    ).astype(jnp.bfloat16)
    values_mine = projected_output[:, QUERY_FEATURES + KEY_FEATURES :].astype(jnp.bfloat16)
    grouped_queries = query_rows.reshape(count_of_rows, KEY_VALUE_HEADS, heads_ratio, HEAD_SIZE)
    key_value = jnp.concatenate([keys_mine.reshape(count_of_rows, KEY_FEATURES), values_mine], 1)

    def masked(block_portion, start_row):
        portion_rows = block_portion.shape[0]
        key_stream, key_segment, unused = positions(lengths, slot_table, start_row, portion_rows)
        key_portion = block_portion[:, :KEY_FEATURES].reshape(
            portion_rows, KEY_VALUE_HEADS, HEAD_SIZE
        )
        value_portion = block_portion[:, KEY_FEATURES:].reshape(
            portion_rows, KEY_VALUE_HEADS, HEAD_SIZE
        )
        scores = (
            jnp.einsum(
                "rgjd,ngd->gjrn", grouped_queries, key_portion, preferred_element_type=jnp.float32
            )
            * score_scale
        )
        allowed = (
            (segment[:, None] == key_segment[None, :]) & (key_stream[None, :] <= stream[:, None])
        )[None, None]
        return (jnp.where(allowed, scores, MASK_FILL), allowed, key_portion, value_portion)

    highest_score = jnp.full((KEY_VALUE_HEADS, heads_ratio, count_of_rows), MASK_FILL, jnp.float32)
    scores, allowed, key_portion, value_portion = masked(
        lax.all_gather(key_value, "ctx", axis=0, tiled=True), jnp.int32(0)
    )
    new_high = jnp.maximum(highest_score, jnp.max(scores, -1))
    weights = jnp.where(allowed, jnp.exp(scores - new_high[..., None]), 0.0)
    weight_sum = jnp.sum(weights, -1)
    gained = jnp.einsum(
        "gjrn,ngd->rgjd",
        weights.astype(jnp.bfloat16),
        value_portion,
        preferred_element_type=jnp.float32,
    )
    accumulated = gained
    highest_score, weight_sum, accumulated = (new_high, weight_sum, accumulated)
    log_total = highest_score + jnp.log(weight_sum)
    attention_output = (
        (accumulated / jnp.transpose(weight_sum, (2, 0, 1))[..., None])
        .astype(jnp.bfloat16)
        .reshape(count_of_rows, QUERY_FEATURES)
    )
    residual = source + full_product(attention_output, out_full)
    scale_two = lax.rsqrt(jnp.mean(residual * residual, -1, keepdims=True) + EPSILON)
    normed_two = (residual * scale_two * gain_two).astype(jnp.bfloat16)
    gate_up_full, down_full = (
        lax.all_gather(w_gate_up, ("dp", "ctx"), axis=0, tiled=True),
        lax.all_gather(w_down, ("dp", "ctx"), axis=0, tiled=True),
    )
    gate_up = full_product(normed_two, gate_up_full)
    gate_part = gate_up[:, :FF]
    up_part = gate_up[:, FF:]
    sigmoid = jax.nn.sigmoid(gate_part)
    hidden = (gate_part * sigmoid * up_part).astype(jnp.bfloat16)
    mlp_term = full_product(hidden, down_full)
    result = (residual + mlp_term).astype(jnp.bfloat16)
    gate_up_full, down_full = (
        lax.all_gather(w_gate_up, ("dp", "ctx"), axis=0, tiled=True),
        lax.all_gather(w_down, ("dp", "ctx"), axis=0, tiled=True),
    )
    grad_hidden = full_back(cotangent, down_full)
    grad_down = jnp.dot(cotangent.T, hidden, preferred_element_type=jnp.float32)
    grad_gate = grad_hidden * up_part * sigmoid * (1.0 + gate_part * (1.0 - sigmoid))
    grad_upper = grad_hidden * gate_part * sigmoid
    grad_gu = jnp.concatenate([grad_gate, grad_upper], 1).astype(jnp.bfloat16)
    grad_normed_two = full_back(grad_gu, gate_up_full)
    grad_w_gate_up = jnp.dot(grad_gu.T, normed_two, preferred_element_type=jnp.float32)
    grad_gain_two = jnp.sum(grad_normed_two * residual * scale_two, 0)
    mlp_owned = owned_three(grad_gain_two, grad_w_gate_up, grad_down)
    grad_residual = cotangent.astype(jnp.float32) + norm_back(
        grad_normed_two, gain_two, residual, scale_two
    )
    grad_res_bf = grad_residual.astype(jnp.bfloat16)
    qkv_full, out_full = (
        lax.all_gather(w_qkv, ("dp", "ctx"), axis=0, tiled=True),
        lax.all_gather(w_out, ("dp", "ctx"), axis=0, tiled=True),
    )
    attention_gradient = full_back(grad_res_bf, out_full).astype(jnp.bfloat16)
    grad_w_out = jnp.dot(grad_res_bf.T, attention_output, preferred_element_type=jnp.float32)
    keys_values_all = lax.all_gather(key_value, "ctx", axis=0, tiled=True)
    grouped_gradient = attention_gradient.reshape(
        count_of_rows, KEY_VALUE_HEADS, heads_ratio, HEAD_SIZE
    )
    attention_grouped = attention_output.reshape(
        count_of_rows, KEY_VALUE_HEADS, heads_ratio, HEAD_SIZE
    )
    row_delta = jnp.transpose(
        jnp.sum(grouped_gradient.astype(jnp.float32) * attention_grouped.astype(jnp.float32), -1),
        (1, 2, 0),
    )
    grouped_rows = keys_values_all.shape[0]
    block_rows = min(512, grouped_rows)
    block_count = grouped_rows // block_rows

    def key_block(grad_queries, which_block):
        start_row = which_block * block_rows
        block_portion = lax.dynamic_slice_in_dim(keys_values_all, start_row, block_rows, 0)
        scores, allowed, key_portion, value_portion = masked(block_portion, start_row)
        weights = jnp.where(allowed, jnp.exp(scores - log_total[..., None]), 0.0)
        grad_values = jnp.einsum(
            "gjrn,rgjd->ngd",
            weights.astype(jnp.bfloat16),
            grouped_gradient,
            preferred_element_type=jnp.float32,
        )
        grad_weights = jnp.einsum(
            "rgjd,ngd->gjrn", grouped_gradient, value_portion, preferred_element_type=jnp.float32
        )
        grad_scores = (weights * (grad_weights - row_delta[..., None])).astype(jnp.bfloat16)
        grad_queries = (
            grad_queries
            + jnp.einsum(
                "gjrn,ngd->rgjd", grad_scores, key_portion, preferred_element_type=jnp.float32
            )
            * score_scale
        )
        grad_keys = (
            jnp.einsum(
                "gjrn,rgjd->ngd", grad_scores, grouped_queries, preferred_element_type=jnp.float32
            )
            * score_scale
        )
        return (
            grad_queries,
            jnp.concatenate(
                [
                    grad_keys.reshape(block_rows, KEY_FEATURES),
                    grad_values.reshape(block_rows, KEY_FEATURES),
                ],
                1,
            ),
        )

    grad_queries, key_terms = lax.scan(
        key_block,
        jnp.zeros((count_of_rows, KEY_VALUE_HEADS, heads_ratio, HEAD_SIZE), jnp.float32),
        jnp.arange(block_count, dtype=jnp.int32),
    )
    key_value_gradient = lax.psum_scatter(
        key_terms.reshape(grouped_rows, 2 * KEY_FEATURES).astype(jnp.bfloat16),
        "ctx",
        scatter_dimension=0,
        tiled=True,
    ).astype(jnp.float32)
    grad_queries = rotate_back(
        grad_queries.reshape(count_of_rows, QUERY_HEADS, HEAD_SIZE), cosine_table, sine_values
    ).reshape(count_of_rows, QUERY_FEATURES)
    grad_keys = rotate_back(
        key_value_gradient[:, :KEY_FEATURES].reshape(count_of_rows, KEY_VALUE_HEADS, HEAD_SIZE),
        cosine_table,
        sine_values,
    ).reshape(count_of_rows, KEY_FEATURES)
    grad_projected = jnp.concatenate(
        [grad_queries, grad_keys, key_value_gradient[:, KEY_FEATURES:]], 1
    ).astype(jnp.bfloat16)
    grad_normed_one = full_back(grad_projected, qkv_full)
    grad_w_qkv = jnp.dot(grad_projected.T, normed_one, preferred_element_type=jnp.float32)
    grad_gain_one = jnp.sum(grad_normed_one * source * scale_one, 0)
    grad_tokens = grad_residual + norm_back(grad_normed_one, gain_one, source, scale_one)
    attn_owned = owned_three(grad_gain_one, grad_w_qkv, grad_w_out)
    return (
        result,
        grad_tokens,
        attn_owned[0],
        attn_owned[1],
        attn_owned[2],
        mlp_owned[0],
        mlp_owned[1],
        mlp_owned[2],
    )


def solution(mesh):
    return jax.shard_map(
        shards,
        mesh=mesh,
        in_specs=(
            P(("dp", "ctx"), None),
            P(("dp", "ctx")),
            P(("dp", "ctx"), None),
            P(("dp", "ctx"), None),
            P(("dp", "ctx")),
            P(("dp", "ctx"), None),
            P(("dp", "ctx"), None),
            P(("dp", "ctx"), None),
            P("dp", None),
            P("dp", None),
        ),
        out_specs=(
            P(("dp", "ctx"), None),
            P(("dp", "ctx"), None),
            P(("dp", "ctx")),
            P(("dp", "ctx"), None),
            P(("dp", "ctx"), None),
            P(("dp", "ctx")),
            P(("dp", "ctx"), None),
            P(("dp", "ctx"), None),
        ),
        check_vma=False,
    )
```

profile of v0, /device:TPU:0, one launch (start us, length us, event | category | flops | bytes accessed | tf_op | source)
XLA Modules:
  0.0 1631.1 jit_solution(5330102366979640390)
XLA Ops:
  10.5 43.5 %all-reduce.5 = (f32[1536]{0:T(1024)S(1)}, f32[1536]{0:T(1024)S(1)}) all-reduce(f32[1536]{0:T(1024)S(1)} %dynamic-update-slice, f32[1536]{0:T(1024)S(1)} %dynamic-update-slice.1), channel_id=1, replica_groups=mesh['dp'=8,'ctx'=4] {'dp','ctx'}, use_global_device_ids=true, to_apply=%add | all-reduce | flops 3072 | bytes 24576
  57.1 38.7 %all-gather.6.cloned.1.call-done = bf16[3072,1536]{1,0:T(8,128)(2,1)} async-done(((bf16[96,1536]{1,0:T(8,128)(2,1)}), bf16[3072,1536]{1,0:T(8,128)(2,1)}) %all-gather.6.cloned.1.call-update) | async-done | bytes 9437200 | tf_op jit(solution)/shard_map/all_gather | solution.py:105
  95.9 5.5 fusion.44
  101.4 1.7 copy-done.12
  107.9 1.6 slice.91
  111.3 20.5 %all-gather.8.cloned.1.call-done = bf16[1024,1536]{1,0:T(8,128)(2,1)} async-done(((bf16[256,1536]{1,0:T(8,128)(2,1)}), bf16[1024,1536]{1,0:T(8,128)(2,1)}) %all-gather.8.cloned.1.call-update) | async-done | bytes 3145744 | tf_op jit(solution)/shard_map/all_gather | solution.py:150
  131.9 2.1 fusion.69
  134.0 1.6 copy.64
  136.4 4.3 fusion.17
  140.7 4.0 fusion.18
  144.8 4.1 fusion.35
  148.9 49.5 %all-gather.10.cloned.1.call-done = bf16[1536,1536]{1,0:T(8,128)(2,1)} async-done(((bf16[48,1536]{1,0:T(8,128)(2,1)}), bf16[1536,1536]{1,0:T(8,128)(2,1)}) %all-gather.10.cloned.1.call-update) | async-done | bytes 4718608 | tf_op jit(solution)/shard_map/all_gather | solution.py:106
  198.4 3.9 multiply_reduce_fusion.3
  202.3 151.2 %all-gather.12.cloned.1.call-done = bf16[8192,1536]{1,0:T(8,128)(2,1)} async-done(((bf16[256,1536]{1,0:T(8,128)(2,1)}), bf16[8192,1536]{1,0:T(8,128)(2,1)}) %all-gather.12.cloned.1.call-update) | async-done | bytes 25165840 | tf_op jit(solution)/shard_map/all_gather | solution.py:173
  353.5 13.7 fusion.66
  367.2 82.5 %all-gather.14.cloned.1.call-done = bf16[1536,4096]{1,0:T(8,128)(2,1)} async-done(((bf16[48,4096]{1,0:T(8,128)(2,1)}), bf16[1536,4096]{1,0:T(8,128)(2,1)}) %all-gather.14.cloned.1.call-update) | async-done | bytes 12582928 | tf_op jit(solution)/shard_map/all_gather | solution.py:174
  449.6 13.2 multiply_convert_fusion.1
  462.9 13.9 multiply_reduce_fusion
  480.9 1.4 multiply_reduce_fusion.1
  482.3 59.7 %while.15 = (s32[]{:T(128)}, f32[256,8,2,96]{0,3,2,1:T(8,128)}, bf16[2,512,1536]{2,1,0:T(8,128)(2,1)}, s32[2]{0:T(128)S(1)}, bf16[1024,1536]{1,0:T(8,128)(2,1)},...) while((s32[]{:T(128)}, f32[256,8,2,96]{0,3,2,1:T(8,128)}, ...), condition=%wide.region_16.17_spmd.clone, body=%wide.region_13.16_spmd.clone.sunk | while | flops 2043966464 | bytes 114495864 | solution.py:260
  483.8 1.5 fusion.123
  485.5 5.7 fusion.124
  491.9 6.7 fusion.127
  498.6 4.3 bitcast_add_fusion.2
  503.8 3.6 fusion.128
  507.4 2.5 bitcast_multiply_fusion.2
  513.3 1.5 fusion.123
  515.0 5.7 fusion.124
  521.4 6.7 fusion.127
  528.1 4.8 bitcast_add_fusion.2
  533.8 3.6 fusion.128
  537.4 2.5 bitcast_multiply_fusion.2
  542.0 4.6 copy.71
  548.3 6.0 fusion.40
  555.1 1.6 add_convert_fusion
  556.9 26.3 %reduce-scatter.8.cloned.1.call-done = bf16[256,1536]{0,1:T(8,128)(2,1)} async-done(((bf16[1024,1536]{0,1:T(8,128)(2,1)}), bf16[256,1536]{0,1:T(8,128)(2,1)}) %reduce-scatter.8.cloned.1.call-update) | async-done | bytes 786448 | tf_op jit(solution)/shard_map/reduce_scatter | solution.py:265
  585.1 9.6 fusion.38
  594.7 14.9 convolution_bitcast_fusion
  609.6 25.3 %copy.83 = f32[1536,4096]{1,0:T(8,128)} copy(f32[1536,4096]{0,1:T(8,128)} %convolution_bitcast_fusion) | data formatting | bytes 50331648
  635.6 22.7 %fusion.23 = f32[8192,1536]{1,0:T(8,128)} fusion(bf16[256,4096]{1,0:T(8,128)(2,1)} %copy-done.14, bf16[256,4096]{1,0:T(8,128)(2,1)} %copy-done.13, f32[256,1536]{1,0:T(8,128)} %copy-done.6, f32[1536]{0:T(1024)S(1)} %copy-done.25, f32[256]{0:T(256)} %copy-done.30), kind=kOutput, calls=%fused_computation.54 | convolution fusion | flops 6452019200 | bytes 56105984 | tf_op jit(solution)/shard_map/dot_general | solution.py:193
  658.4 10.2 fusion.25
  668.6 8.5 fusion.34
  677.1 41.0 %all-reduce.4 = (f32[1536]{0:T(1024)S(1)}, f32[1536]{0:T(1024)S(1)}) all-reduce(f32[1536]{0:T(1024)} %get-tuple-element.305, f32[1536]{0:T(1024)} %get-tuple-element.303), channel_id=3, replica_groups=mesh['dp'=8,'ctx'=4] {'dp','ctx'}, use_global_device_ids=true, to_apply=%region_20.21.clone | all-reduce | flops 3072 | bytes 24576
  719.9 3.0 fusion.31
  722.9 3.4 reduce-scatter.12.cloned.1.call-done
  726.3 212.8 %reduce-scatter.10.cloned.1.call-done = f32[96,1536]{1,0:T(8,128)} async-done(((f32[3072,1536]{1,0:T(8,128)}), f32[96,1536]{1,0:T(8,128)}) %reduce-scatter.10.cloned.1.call-update) | async-done | bytes 589840 | tf_op jit(solution)/shard_map/reduce_scatter | solution.py:82
  939.1 249.2 %reduce-scatter.16.cloned.1.call-done = f32[48,4096]{1,0:T(8,128)} async-done(((f32[1536,4096]{1,0:T(8,128)}), f32[48,4096]{1,0:T(8,128)}) %reduce-scatter.16.cloned.1.call-update) | async-done | bytes 786448
  1188.3 435.5 %reduce-scatter.14.cloned.1.call-done = f32[256,1536]{1,0:T(8,128)} async-done(((f32[8192,1536]{1,0:T(8,128)}), f32[256,1536]{1,0:T(8,128)}) %reduce-scatter.14.cloned.1.call-update) | async-done | bytes 1572880 | tf_op jit(solution)/shard_map/reduce_scatter | solution.py:82
  (165 shorter events, 33.9 us)
Async XLA Ops:
  7.2 88.7 %all-gather.6.cloned.1.call-start = ((), (), s32[]{:S(2)}) async-start(), calls=%async_computation.5 | async-start | bytes 9732096 | tf_op jit(solution)/shard_map/all_gather | solution.py:105
  7.9 124.0 %all-gather.8.cloned.1.call-start = ((), (), s32[]{:S(2)}) async-start(), calls=%async_computation.6 | async-start | bytes 3932160 | tf_op jit(solution)/shard_map/all_gather | solution.py:150
  54.0 47.3 %copy-start.22 = (f32[1536]{0:T(1024)}, f32[1536]{0:T(1024)S(1)}, u32[]{:S(2)}) copy-start(f32[1536]{0:T(1024)S(1)} %get-tuple-element.337) | copy-start | bytes 18436
  54.0 422.7 %copy-start.24 = (f32[1536]{0:T(1024)}, f32[1536]{0:T(1024)S(1)}, u32[]{:S(2)}) copy-start(f32[1536]{0:T(1024)S(1)} %get-tuple-element.338) | copy-start | bytes 18436
  56.8 44.5 %copy-start.27 = (f32[256]{0:T(256)}, f32[256]{0:T(256)S(1)}, u32[]{:S(2)}) copy-start(f32[256]{0:T(256)S(1)} %get-tuple-element.359) | copy-start | bytes 3076
  57.1 52.8 %copy-start.18 = (f32[256,48]{0,1:T(8,128)}, f32[256,48]{0,1:T(8,128)S(1)}, u32[]{:S(2)}) copy-start(f32[256,48]{0,1:T(8,128)S(1)} %get-tuple-element.356) | copy-start | bytes 147460
  57.1 52.8 %copy-start.20 = (f32[256,48]{0,1:T(8,128)}, f32[256,48]{0,1:T(8,128)S(1)}, u32[]{:S(2)}) copy-start(f32[256,48]{0,1:T(8,128)S(1)} %get-tuple-element.357) | copy-start | bytes 147460
  101.3 1.7 copy-start.12
  103.5 3.7 copy-start.32
  103.5 3.8 copy-start.26
  104.7 93.7 %all-gather.10.cloned.1.call-start = ((), (), s32[]{:S(2)}) async-start(), calls=%async_computation.7 | async-start | bytes 4866048 | tf_op jit(solution)/shard_map/all_gather | solution.py:106
  105.4 248.1 %all-gather.12.cloned.1.call-start = ((), (), s32[]{:S(2)}) async-start(), calls=%async_computation.8 | async-start | bytes 25952256 | tf_op jit(solution)/shard_map/all_gather | solution.py:173
  106.0 343.6 %all-gather.14.cloned.1.call-start = ((), (), s32[]{:S(2)}) async-start(), calls=%async_computation.9 | async-start | bytes 12976128 | tf_op jit(solution)/shard_map/all_gather | solution.py:174
  106.6 476.6 %reduce-scatter.8.cloned.1.call-start = ((), (), s32[]{:S(2)}) async-start(), calls=%async_computation.10 | async-start | bytes 3932160 | tf_op jit(solution)/shard_map/reduce_scatter | solution.py:265
  110.2 1.1 copy-start.7
  110.2 1.1 copy-start.8
  140.7 4.1 copy-start.15
  144.8 53.6 %copy-start.4 = (bf16[256,1536]{1,0:T(8,128)(2,1)S(1)}, bf16[256,1536]{1,0:T(8,128)(2,1)}, u32[]{:S(2)}) copy-start(bf16[256,1536]{1,0:T(8,128)(2,1)} %param.12) | copy-start | bytes 2359300
  148.9 332.0 %copy-start.9 = (bf16[256,8,2,96]{0,3,2,1:T(8,128)(2,1)}, bf16[256,8,2,96]{0,3,2,1:T(8,128)(2,1)S(1)}, u32[]{:S(2)}) copy-start(bf16[256,8,2,96]{0,3,2,1:T(8,128)(2,1)S(1)} %fusion.35) | copy-start | bytes 2359300
  202.2 274.5 %copy-start.6 = (f32[256,1536]{1,0:T(8,128)}, f32[256,1536]{1,0:T(8,128)S(1)}, u32[]{:S(2)}) copy-start(f32[256,1536]{1,0:T(8,128)S(1)} %get-tuple-element.365) | copy-start | bytes 4718596
  202.3 274.5 %copy-start.30 = (f32[256]{0:T(256)}, f32[256]{0:T(256)S(1)}, u32[]{:S(2)}) copy-start(f32[256]{0:T(256)S(1)} %get-tuple-element.361) | copy-start | bytes 3076
  353.5 96.1 %copy-start.11 = (bf16[256,1536]{1,0:T(8,128)(2,1)S(1)}, bf16[256,1536]{1,0:T(8,128)(2,1)}, u32[]{:S(2)}) copy-start(bf16[256,1536]{1,0:T(8,128)(2,1)} %param.19) | copy-start | bytes 2359300
  449.6 28.7 %slice-start = ((s8[4718592]{0:T(1024)(128)(4,1)}), s8[4194304]{0:T(1024)(128)(4,1)S(1)}, s32[]{:S(2)}) async-start(s8[4718592]{0:T(1024)(128)(4,1)} %bitcast.195), calls=%async_computation.15 | async-start | bytes 8388608
  462.9 13.9 copy-start.13
  462.9 13.9 copy-start.14
  462.9 15.5 slice-start.1
  477.2 1.1 copy-start.2
  498.6 5.2 copy-start.1
  503.8 3.6 copy-start
  528.1 5.7 copy-start.1
  533.8 3.6 copy-start
  546.7 1.4 copy-start.3
  546.7 1.6 copy-start.10
  546.7 179.6 %reduce-scatter.12.cloned.1.call-start = ((), (), s32[]{:S(2)}) async-start(), calls=%async_computation.12 | async-start | bytes 9732096 | tf_op jit(solution)/shard_map/reduce_scatter | solution.py:83
  554.3 0.8 copy-start.19
  554.3 0.8 copy-start.21
  554.3 384.8 %reduce-scatter.10.cloned.1.call-start = ((), (), s32[]{:S(2)}) async-start(), calls=%async_computation.11 | async-start | bytes 19464192 | tf_op jit(solution)/shard_map/reduce_scatter | solution.py:82
  556.8 28.3 %copy-start.5 = (bf16[256,1536]{1,0:T(8,128)(2,1)S(1)}, bf16[256,1536]{1,0:T(8,128)(2,1)}, u32[]{:S(2)}) copy-start(bf16[256,1536]{1,0:T(8,128)(2,1)} %param.12) | copy-start | bytes 2359300
  556.8 28.2 %copy-start.23 = (f32[1536]{0:T(1024)S(1)}, f32[1536]{0:T(1024)}, u32[]{:S(2)}) copy-start(f32[1536]{0:T(1024)} %copy-done.22) | copy-start | bytes 18436
  556.9 28.2 %copy-start.28 = (f32[256]{0:T(256)S(1)}, f32[256]{0:T(256)}, u32[]{:S(2)}) copy-start(f32[256]{0:T(256)} %copy-done.27) | copy-start | bytes 3076
  584.3 0.8 copy-start.16
  594.7 593.6 %reduce-scatter.16.cloned.1.call-start = ((), (), s32[]{:S(2)}) async-start(), calls=%async_computation.14 | async-start | bytes 25952256
  634.9 0.7 copy-start.25
  635.0 988.9 %reduce-scatter.14.cloned.1.call-start = ((), (), s32[]{:S(2)}) async-start(), calls=%async_computation.13 | async-start | bytes 51904512 | tf_op jit(solution)/shard_map/reduce_scatter | solution.py:82
  658.4 10.2 copy-start.17
  658.4 10.2 copy-start.29
  668.6 51.4 %copy-start.31 = (f32[256]{0:T(256)S(1)}, f32[256]{0:T(256)}, u32[]{:S(2)}) copy-start(f32[256]{0:T(256)} %get-tuple-element.358) | copy-start | bytes 3076
Sparse Core Ops, SparseCore 0:
  10.9 84.9 all-gather.5
  104.8 27.0 all-gather.7
  134.8 63.5 all-gather.9
  201.1 152.3 all-gather.11
  356.2 93.3 all-gather.13
  546.8 36.2 reduce-scatter.7
  589.6 136.6 reduce-scatter.11
  733.3 205.7 reduce-scatter.9
  946.1 242.1 reduce-scatter.15
  1195.1 428.6 reduce-scatter.13
where the time goes:
time: 1640 us; the launch traced here: 1630 us
  waiting for transfers between devices  1270 us (77%)
  matrix products  178 us (11%)
  blocking collectives  84.6 us (5%)
  local copies, waits for them, and re-layouts  59.6 us (4%)
  other arithmetic  19.4 us (1%)
    reduce_scatter x2, waiting for transfers between devices, owned_three(): lax.psum_scatter(second_part, ('dp', 'ctx'), scatter_dimension=0, tiled=T...  648 us
    unnamed x11, waiting for transfers between devices  252 us
    all_gather x1, waiting for transfers between devices, shards(): lax.all_gather(w_gate_up, ('dp', 'ctx'), axis=0, tiled=True)  151 us
    unnamed x2, blocking collectives  84.6 us
    all_gather x1, waiting for transfers between devices, shards(): lax.all_gather(w_down, ('dp', 'ctx'), axis=0, tiled=True)  82.5 us
    all_gather x1, waiting for transfers between devices, shards(): lax.all_gather(w_out, ('dp', 'ctx'), axis=0, tiled=True)  49.5 us
    all_gather x1, waiting for transfers between devices, shards(): lax.all_gather(w_qkv, ('dp', 'ctx'), axis=0, tiled=True)  38.7 us
    dot_general x4, matrix products, full_back(): return jnp.dot(grad_side, whole_weight, preferred_element_type=jnp.float32)  37 us
  transfers between devices with their start and end apart: 10, of which 10 were waited for; matrix products, arithmetic and copies ran while one was open for 9% of the time, Pallas kernels for 0%

commit v1 on v0

--- a/solution.py
+++ b/solution.py
@@ -14,6 +14,12 @@
 EPSILON = 1e-05
 THETA = 100000.0
 MASK_FILL = -1e30
+
+
+def tiled_gather(x, axis, dim):
+    size = lax.axis_size(axis)
+    repeats = [size if d == dim else 1 for d in range(x.ndim)]
+    return lax.all_to_all(jnp.tile(x, repeats), axis, split_axis=dim, concat_axis=dim, tiled=True)
 
 
 def rope_tables(rope_pos):
@@ -170,7 +176,7 @@
     scale_two = lax.rsqrt(jnp.mean(residual * residual, -1, keepdims=True) + EPSILON)
     normed_two = (residual * scale_two * gain_two).astype(jnp.bfloat16)
     gate_up_full, down_full = (
-        lax.all_gather(w_gate_up, ("dp", "ctx"), axis=0, tiled=True),
+        tiled_gather(w_gate_up, ("dp", "ctx"), 0),
         lax.all_gather(w_down, ("dp", "ctx"), axis=0, tiled=True),
     )
     gate_up = full_product(normed_two, gate_up_full)

time: 1640 us -> 2080 us (1.27)
  waiting for transfers between devices: 1270 us -> 1700 us
    all_to_all x0 -> x1, waiting for transfers between devices: none -> 438 us  [tiled_gather(): lax.all_to_all(jnp.tile(x, repeats), axis, split_axis=dim, concat_axis=di...]
    all_gather x1, waiting for transfers between devices: 49.5 us -> 243 us  [shards(): lax.all_gather(w_out, ('dp', 'ctx'), axis=0, tiled=True)]
    all_gather x1, waiting for transfers between devices: 151 us -> 0.01 us  [shards(): lax.all_gather(w_gate_up, ('dp', 'ctx'), axis=0, tiled=True)]
    all_gather x1, waiting for transfers between devices: 82.5 us -> 0.01 us  [shards(): lax.all_gather(w_down, ('dp', 'ctx'), axis=0, tiled=True)]
  transfers between devices with their start and end apart: 10 -> 11, of which waited for: 10 -> 9; matrix products, arithmetic and copies ran while one was open for 9% -> 8% of each run, Pallas kernels for 0% -> 0%
where the time goes in v1:
time: 2080 us
  waiting for transfers between devices  1700 us (82%)
  matrix products  180 us (9%)
  blocking collectives  84.5 us (4%)
  local copies, waits for them, and re-layouts  68.7 us (3%)
    reduce_scatter x2, waiting for transfers between devices, owned_three(): lax.psum_scatter(second_part, ('dp', 'ctx'), scatter_dimension=0, tiled=T...  648 us
    all_to_all x1, waiting for transfers between devices, tiled_gather(): lax.all_to_all(jnp.tile(x, repeats), axis, split_axis=dim, concat_axis=di...  438 us
    unnamed x11, waiting for transfers between devices  252 us
    all_gather x1, waiting for transfers between devices, shards(): lax.all_gather(w_out, ('dp', 'ctx'), axis=0, tiled=True)  243 us
    unnamed x2, blocking collectives  84.5 us
    reduce_scatter x1, waiting for transfers between devices, shards(): lax.psum_scatter(key_terms.reshape(grouped_rows, 2 * KEY_FEATURES).astype...  46.7 us
  transfers between devices with their start and end apart: 11, of which 9 were waited for; matrix products, arithmetic and copies ran while one was open for 8% of the time, Pallas kernels for 0%

profile of v1, /device:TPU:0, one launch (start us, length us, event | category | flops | bytes accessed | tf_op | source)
XLA Modules:
  0.0 2077.1 jit_solution(1028406205708396951)
XLA Ops:
  10.5 43.5 %all-reduce.5 = (f32[1536]{0:T(1024)S(1)}, f32[1536]{0:T(1024)S(1)}) all-reduce(f32[1536]{0:T(1024)S(1)} %dynamic-update-slice, f32[1536]{0:T(1024)S(1)} %dynamic-update-slice.1), channel_id=1, replica_groups=mesh['dp'=8,'ctx'=4] {'dp','ctx'}, use_global_device_ids=true, to_apply=%add | all-reduce | flops 3072 | bytes 24576
  57.2 38.7 %all-gather.6.cloned.1.call-done = bf16[3072,1536]{1,0:T(8,128)(2,1)} async-done(((bf16[96,1536]{1,0:T(8,128)(2,1)}), bf16[3072,1536]{1,0:T(8,128)(2,1)}) %all-gather.6.cloned.1.call-update) | async-done | bytes 9437200 | tf_op jit(solution)/shard_map/all_gather | solution.py:111
  95.8 5.5 fusion.44
  101.3 1.7 copy-done.13
  106.0 9.1 tile.2
  115.0 4.3 all-to-all-start
  121.2 1.5 slice.91
  124.6 33.7 %all-gather.8.cloned.1.call-done = bf16[1024,1536]{1,0:T(8,128)(2,1)} async-done(((bf16[256,1536]{1,0:T(8,128)(2,1)}), bf16[1024,1536]{1,0:T(8,128)(2,1)}) %all-gather.8.cloned.1.call-update) | async-done | bytes 3145744 | tf_op jit(solution)/shard_map/all_gather | solution.py:156
  158.2 2.1 fusion.69
  160.3 1.6 copy.64
  162.7 4.3 fusion.17
  167.1 4.0 fusion.18
  171.1 4.1 fusion.35
  175.3 242.8 %all-gather.10.cloned.1.call-done = bf16[1536,1536]{1,0:T(8,128)(2,1)} async-done(((bf16[48,1536]{1,0:T(8,128)(2,1)}), bf16[1536,1536]{1,0:T(8,128)(2,1)}) %all-gather.10.cloned.1.call-update) | async-done | bytes 4718608 | tf_op jit(solution)/shard_map/all_gather | solution.py:112
  418.0 3.9 multiply_reduce_fusion.3
  421.9 437.6 %all-to-all-done = bf16[32,256,1536]{2,1,0:T(8,128)(2,1)} async-done(((bf16[32,256,1536]{2,1,0:T(8,128)(2,1)}), bf16[32,256,1536]{2,1,0:T(8,128)(2,1)}, u32[]{:S(2)}, u32[]{:S(2)}) %all-to-all-start) | async-done | bytes 25165856 | tf_op jit(solution)/shard_map/all_to_all | solution.py:22
  859.5 14.1 fusion.66
  873.6 13.7 multiply_convert_fusion.1
  887.3 13.6 multiply_reduce_fusion
  902.5 3.7 convolution_convert_fusion
  908.8 59.8 %while.15 = (s32[]{:T(128)}, f32[256,8,2,96]{0,3,2,1:T(8,128)}, bf16[2,512,1536]{2,1,0:T(8,128)(2,1)}, s32[2]{0:T(128)S(1)}, bf16[1024,1536]{1,0:T(8,128)(2,1)},...) while((s32[]{:T(128)}, f32[256,8,2,96]{0,3,2,1:T(8,128)}, ...), condition=%wide.region_16.17_spmd.clone, body=%wide.region_13.16_spmd.clone.sunk | while | flops 2043966464 | bytes 114495864 | solution.py:266
  910.3 1.5 fusion.123
  912.0 5.7 fusion.124
  918.4 6.7 fusion.127
  925.1 4.3 bitcast_add_fusion.2
  930.3 3.6 fusion.128
  933.9 2.5 bitcast_multiply_fusion.2
  941.6 5.7 fusion.124
  947.9 6.7 fusion.127
  954.6 4.8 bitcast_add_fusion.2
  960.3 3.6 fusion.128
  963.9 2.5 bitcast_multiply_fusion.2
  968.6 4.6 copy.71
  974.9 5.1 fusion.40
  980.7 1.6 add_convert_fusion
  982.4 46.7 %reduce-scatter.8.cloned.1.call-done = bf16[256,1536]{0,1:T(8,128)(2,1)} async-done(((bf16[1024,1536]{0,1:T(8,128)(2,1)}), bf16[256,1536]{0,1:T(8,128)(2,1)}) %reduce-scatter.8.cloned.1.call-update) | async-done | bytes 786448 | tf_op jit(solution)/shard_map/reduce_scatter | solution.py:271
  1031.1 9.6 fusion.38
  1040.7 14.9 convolution_bitcast_fusion
  1055.6 25.4 %copy.83 = f32[1536,4096]{1,0:T(8,128)} copy(f32[1536,4096]{0,1:T(8,128)} %convolution_bitcast_fusion) | data formatting | bytes 50331648
  1081.7 22.7 %fusion.23 = f32[8192,1536]{1,0:T(8,128)} fusion(bf16[256,4096]{1,0:T(8,128)(2,1)} %get-tuple-element.342, bf16[256,4096]{1,0:T(8,128)(2,1)} %get-tuple-element.341, f32[256,1536]{1,0:T(8,128)} %copy-done.6, f32[1536]{0:T(1024)S(1)} %copy-done.24, f32[256]{0:T(256)} %copy-done.29), kind=kOutput, calls=%fused_computation.54 | convolution fusion | flops 6452019200 | bytes 56105984 | tf_op jit(solution)/shard_map/dot_general | solution.py:199
  1104.5 10.2 fusion.25
  1114.6 8.5 fusion.34
  1123.2 41.0 %all-reduce.4 = (f32[1536]{0:T(1024)S(1)}, f32[1536]{0:T(1024)S(1)}) all-reduce(f32[1536]{0:T(1024)} %get-tuple-element.305, f32[1536]{0:T(1024)} %get-tuple-element.303), channel_id=3, replica_groups=mesh['dp'=8,'ctx'=4] {'dp','ctx'}, use_global_device_ids=true, to_apply=%region_20.21.clone | all-reduce | flops 3072 | bytes 24576
  1166.0 3.0 fusion.31
  1169.0 3.3 reduce-scatter.12.cloned.1.call-done
  1172.3 212.8 %reduce-scatter.10.cloned.1.call-done = f32[96,1536]{1,0:T(8,128)} async-done(((f32[3072,1536]{1,0:T(8,128)}), f32[96,1536]{1,0:T(8,128)}) %reduce-scatter.10.cloned.1.call-update) | async-done | bytes 589840 | tf_op jit(solution)/shard_map/reduce_scatter | solution.py:88
  1385.1 249.1 %reduce-scatter.16.cloned.1.call-done = f32[48,4096]{1,0:T(8,128)} async-done(((f32[1536,4096]{1,0:T(8,128)}), f32[48,4096]{1,0:T(8,128)}) %reduce-scatter.16.cloned.1.call-update) | async-done | bytes 786448
  1634.2 435.6 %reduce-scatter.14.cloned.1.call-done = f32[256,1536]{1,0:T(8,128)} async-done(((f32[8192,1536]{1,0:T(8,128)}), f32[256,1536]{1,0:T(8,128)}) %reduce-scatter.14.cloned.1.call-update) | async-done | bytes 1572880 | tf_op jit(solution)/shard_map/reduce_scatter | solution.py:88
  (161 shorter events, 35.5 us)
Async XLA Ops:
  7.2 88.6 %all-gather.6.cloned.1.call-start = ((), (), s32[]{:S(2)}) async-start(), calls=%async_computation.6 | async-start | bytes 9732096 | tf_op jit(solution)/shard_map/all_gather | solution.py:111
  7.9 150.3 %all-gather.8.cloned.1.call-start = ((), (), s32[]{:S(2)}) async-start(), calls=%async_computation.7 | async-start | bytes 3932160 | tf_op jit(solution)/shard_map/all_gather | solution.py:156
  54.0 47.2 %copy-start.21 = (f32[1536]{0:T(1024)}, f32[1536]{0:T(1024)S(1)}, u32[]{:S(2)}) copy-start(f32[1536]{0:T(1024)S(1)} %get-tuple-element.337) | copy-start | bytes 18436
  54.0 846.9 %copy-start.23 = (f32[1536]{0:T(1024)}, f32[1536]{0:T(1024)S(1)}, u32[]{:S(2)}) copy-start(f32[1536]{0:T(1024)S(1)} %get-tuple-element.338) | copy-start | bytes 18436
  56.9 44.4 %copy-start.26 = (f32[256]{0:T(256)}, f32[256]{0:T(256)S(1)}, u32[]{:S(2)}) copy-start(f32[256]{0:T(256)S(1)} %get-tuple-element.359) | copy-start | bytes 3076
  57.1 66.1 %copy-start.17 = (f32[256,48]{0,1:T(8,128)}, f32[256,48]{0,1:T(8,128)S(1)}, u32[]{:S(2)}) copy-start(f32[256,48]{0,1:T(8,128)S(1)} %get-tuple-element.356) | copy-start | bytes 147460
  57.1 66.1 %copy-start.19 = (f32[256,48]{0,1:T(8,128)}, f32[256,48]{0,1:T(8,128)S(1)}, u32[]{:S(2)}) copy-start(f32[256,48]{0,1:T(8,128)S(1)} %get-tuple-element.357) | copy-start | bytes 147460
  101.3 1.7 copy-start.13
  103.5 2.5 copy-start.9
  104.6 313.4 %all-gather.10.cloned.1.call-start = ((), (), s32[]{:S(2)}) async-start(), calls=%async_computation.8 | async-start | bytes 4866048 | tf_op jit(solution)/shard_map/all_gather | solution.py:112
  105.4 768.2 %all-gather.12.cloned.1.call-start = ((), (), s32[]{:S(2)}) async-start(), calls=%async_computation.9 | async-start | bytes 12976128 | tf_op jit(solution)/shard_map/all_gather | solution.py:180
  115.0 5.5 copy-start.31
  115.0 5.6 copy-start.25
  115.0 744.5 %all-to-all-start = ((bf16[32,256,1536]{2,1,0:T(8,128)(2,1)}), bf16[32,256,1536]{2,1,0:T(8,128)(2,1)}, u32[]{:S(2)}, u32[]{:S(2)}) async-start(bf16[32,256,1536]{2,1,0:T(8,128)(2,1)} %tile.2), calls=%async_computation | async-start | bytes 50331648 | tf_op jit(solution)/shard_map/all_to_all | solution.py:22
  119.3 768.0 %all-gather.14.cloned.1.call-start = ((), (), s32[]{:S(2)}) async-start(), calls=%async_computation.10 | async-start | bytes 25952256 | tf_op jit(solution)/shard_map/all_gather | solution.py:190
  119.9 909.3 %reduce-scatter.8.cloned.1.call-start = ((), (), s32[]{:S(2)}) async-start(), calls=%async_computation.11 | async-start | bytes 3932160 | tf_op jit(solution)/shard_map/reduce_scatter | solution.py:271
  123.4 1.1 copy-start.7
  123.5 1.1 copy-start.8
  167.1 4.1 copy-start.14
  171.1 246.9 %copy-start.4 = (bf16[256,1536]{1,0:T(8,128)(2,1)S(1)}, bf16[256,1536]{1,0:T(8,128)(2,1)}, u32[]{:S(2)}) copy-start(bf16[256,1536]{1,0:T(8,128)(2,1)} %param.12) | copy-start | bytes 2359300
  175.2 732.1 %copy-start.10 = (bf16[256,8,2,96]{0,3,2,1:T(8,128)(2,1)}, bf16[256,8,2,96]{0,3,2,1:T(8,128)(2,1)S(1)}, u32[]{:S(2)}) copy-start(bf16[256,8,2,96]{0,3,2,1:T(8,128)(2,1)S(1)} %fusion.35) | copy-start | bytes 2359300
  421.9 479.0 %copy-start.6 = (f32[256,1536]{1,0:T(8,128)}, f32[256,1536]{1,0:T(8,128)S(1)}, u32[]{:S(2)}) copy-start(f32[256,1536]{1,0:T(8,128)S(1)} %get-tuple-element.365) | copy-start | bytes 4718596
  421.9 479.0 %copy-start.29 = (f32[256]{0:T(256)}, f32[256]{0:T(256)S(1)}, u32[]{:S(2)}) copy-start(f32[256]{0:T(256)S(1)} %get-tuple-element.361) | copy-start | bytes 3076
  859.5 14.1 copy-start.12
  901.4 1.1 copy-start.2
  925.1 5.2 copy-start.1
  930.3 3.6 copy-start
  954.6 5.7 copy-start.1
  960.3 3.6 copy-start
  973.3 1.4 copy-start.3
  973.3 1.6 copy-start.11
  973.3 199.0 %reduce-scatter.12.cloned.1.call-start = ((), (), s32[]{:S(2)}) async-start(), calls=%async_computation.13 | async-start | bytes 9732096 | tf_op jit(solution)/shard_map/reduce_scatter | solution.py:89
  979.9 0.8 copy-start.18
  979.9 0.8 copy-start.20
  980.0 405.1 %reduce-scatter.10.cloned.1.call-start = ((), (), s32[]{:S(2)}) async-start(), calls=%async_computation.12 | async-start | bytes 19464192 | tf_op jit(solution)/shard_map/reduce_scatter | solution.py:88
  982.4 48.7 %copy-start.5 = (bf16[256,1536]{1,0:T(8,128)(2,1)S(1)}, bf16[256,1536]{1,0:T(8,128)(2,1)}, u32[]{:S(2)}) copy-start(bf16[256,1536]{1,0:T(8,128)(2,1)} %param.12) | copy-start | bytes 2359300
  982.4 48.7 %copy-start.22 = (f32[1536]{0:T(1024)S(1)}, f32[1536]{0:T(1024)}, u32[]{:S(2)}) copy-start(f32[1536]{0:T(1024)} %copy-done.21) | copy-start | bytes 18436
  982.4 48.7 %copy-start.27 = (f32[256]{0:T(256)S(1)}, f32[256]{0:T(256)}, u32[]{:S(2)}) copy-start(f32[256]{0:T(256)} %copy-done.26) | copy-start | bytes 3076
  1030.3 0.8 copy-start.15
  1040.7 593.5 %reduce-scatter.16.cloned.1.call-start = ((), (), s32[]{:S(2)}) async-start(), calls=%async_computation.15 | async-start | bytes 25952256
  1081.0 0.7 copy-start.24
  1081.0 988.8 %reduce-scatter.14.cloned.1.call-start = ((), (), s32[]{:S(2)}) async-start(), calls=%async_computation.14 | async-start | bytes 51904512 | tf_op jit(solution)/shard_map/reduce_scatter | solution.py:88
  1104.4 10.2 copy-start.16
  1104.4 10.2 copy-start.28
  1114.6 51.4 %copy-start.30 = (f32[256]{0:T(256)S(1)}, f32[256]{0:T(256)}, u32[]{:S(2)}) copy-start(f32[256]{0:T(256)} %get-tuple-element.358) | copy-start | bytes 3076
Sparse Core Ops, SparseCore 0:
  10.9 84.8 all-gather.5
  104.8 53.4 all-gather.7
  161.2 256.8 all-gather.9
  420.8 211.0 all-gather.11
  634.6 239.3 all-gather.13
  973.4 55.7 reduce-scatter.7
  1035.6 136.6 reduce-scatter.11
  1179.3 205.7 reduce-scatter.9
  1392.1 242.0 reduce-scatter.15
  1641.1 428.6 reduce-scatter.13
